TPU v7x, 32 devices: a whole 2x2x4 slice. The times are simulated.
32 devices in a mesh: groups: 2 (over y), expert: 8 (over z, core), dp: 2 (over x).
Axes of the slice: x: 2, y: 2, z: 4, core: 2. Of those that a mesh axis runs over, the one named last changes fastest.
Arguments:
- tokens: bfloat16 [1024, 2048], P(('groups', 'expert'), 'dp'), parts along dimension 0, may hold values from -6 to 6
- expert_ids: int32 [1024, 8], P(('groups', 'expert')), parts along dimension 0, may hold values from 0 to 15, all different within a row; in each aligned block of 64 rows (0 to 63, 64 to 127, ...) at most 64 rows name the same one
- gate_levels: int32 [1024, 8], P(('groups', 'expert')), parts along dimension 0, may hold values from 1 to 255
- gate_weight: bfloat16 [16, 2048, 1536], P('expert', None, 'dp'), may hold values from -0.125 to 0.125
- up_weight: bfloat16 [16, 2048, 1536], P('expert', None, 'dp'), may hold values from -0.125 to 0.125
- down_weight: bfloat16 [16, 1536, 2048], P('expert', None, 'dp'), may hold values from -0.15625 to 0.15625
Outputs:
- mixed: bfloat16 [1024, 2048], P(('groups', 'expert'), 'dp'), parts along dimension 0
There are 2 independent parts, one for each index of `groups`. A program takes and returns all parts, laid end to end along the dimension named above; an argument that names none is the same for every part. Nothing has to cross between parts.
Inputs may be any that keep to these rules, and one draw needn't show every extreme that they name: `expert_ids`: each row names 8 different experts. Among the rows of one index of the expert axis no expert is named more than 64 times, a bound that some block reaches.
All inputs are finite; a program needn't handle non-finite values.
Results may differ from a plain program's by a relative error of at most 0.0057.
Values may be sent and summed in bfloat16 or wider, within the bound.
A program may use at most 64 MiB of HBM per device.

v0:
```python
import functools

import jax
import jax.numpy as jnp
from jax import lax
from jax.experimental import pallas as pl
from jax.experimental.pallas import tpu as pltpu
from jax.sharding import PartitionSpec as P

MESH = pl.DeviceIdType.MESH
WIDE = 256


def slot_numbers(chosen_ids, experts, capacity):
    flat_ids = chosen_ids.reshape(-1)
    labels = jnp.arange(experts, dtype=jnp.int32)
    onehot = (flat_ids[:, None] == labels[None, :]).astype(jnp.int32)
    before = jnp.cumsum(onehot, axis=0) - onehot
    position = jnp.sum(before * onehot, axis=1)
    return (flat_ids * capacity + position).reshape(chosen_ids.shape)


def route_matrix(slots, count):
    targets = jnp.arange(count, dtype=jnp.int32)
    return jnp.any(targets[:, None, None] == slots[None, :, :], axis=2).astype(jnp.bfloat16)


def routed_on_device(tokens, expert_ids, gate_levels, gate_weight, up_weight, down_weight):
    tok_dev = tokens.shape[0]
    picks = expert_ids.shape[1]
    exp_dev = gate_weight.shape[0]
    n_expert = lax.axis_size("expert")
    experts = exp_dev * n_expert
    capacity = min(tok_dev, max(2, 2 * tok_dev * picks // experts))
    slot_count = experts * capacity
    own_slots = slot_numbers(expert_ids, experts, capacity)
    route = route_matrix(own_slots, slot_count)
    whole = lax.all_gather(tokens, "dp", axis=1, tiled=True)
    outgoing = jnp.dot(route, whole, preferred_element_type=jnp.float32).astype(jnp.bfloat16)
    outgoing = outgoing.reshape(n_expert, exp_dev, capacity, whole.shape[1])
    arrived = lax.all_to_all(outgoing, "expert", split_axis=0, concat_axis=0, tiled=True)
    gate_part = jnp.einsum(
        "sxcd,xdf->sxcf", arrived, gate_weight, preferred_element_type=jnp.float32
    )
    up_part = jnp.einsum("sxcd,xdf->sxcf", arrived, up_weight, preferred_element_type=jnp.float32)
    hidden = (jax.nn.silu(gate_part) * up_part).astype(jnp.bfloat16)
    out_features = down_weight.shape[2]
    outputs = jnp.einsum(
        "sxcf,xfk->sxck",
        lax.all_gather(hidden, "dp", axis=3, tiled=True),
        down_weight,
        preferred_element_type=jnp.float32,
    )
    result = outputs.astype(jnp.bfloat16)
    returned = lax.all_to_all(result, "expert", split_axis=0, concat_axis=0, tiled=True)
    returned = returned.reshape(slot_count, out_features)
    shares = gate_levels.astype(jnp.float32) / 256.0
    targets = jnp.arange(slot_count, dtype=jnp.int32)
    weighting = jnp.sum(
        jnp.where(
            targets[None, :, None] == own_slots[:, None, :], shares[:, None, :], jnp.float32(0.0)
        ),
        axis=2,
    )
    weighting = weighting.astype(jnp.bfloat16)
    combined = jnp.dot(weighting, returned, preferred_element_type=jnp.float32)
    return combined.astype(jnp.bfloat16)


def visit_order(chips):
    table = []
    for z in range(chips):
        near = sorted(range(chips), key=lambda q: (abs(q - z), q if 2 * z < chips else -q))
        if 0 < z < chips - 1:
            near = near[:1] + near[2:] + near[1:2]
        else:
            near = near[:-2] + [near[-1], near[-2]]
        table.append(near)
    return table


def dense_kernel(
    chips, tok_hbm, ids_hbm, levels_hbm, gate_hbm, up_hbm, down_hbm, out,
    ids, levels, gate_w, up_w, down_w, x_buf, s_buf, hid, part, pair_out, pair_in, ret_out, ret_in, total,
    i_sem, w_sem, x_send, x_recv, t_send, h_send, h_recv, p_send, p_recv, r_send, r_recv,
):
    e = lax.axis_index("expert")
    d = lax.axis_index("dp")
    z, c = lax.div(e, 2), lax.rem(e, 2)
    rows = tok_hbm.shape[0]
    exp_dev, depth, ff = gate_w.shape
    half = depth // 2
    width = down_w.shape[2]
    mate = z * 2 + 1 - c

    barrier = pltpu.get_barrier_semaphore()
    pl.semaphore_signal(barrier, inc=1, device_id={"dp": 1 - d}, device_id_type=MESH)
    pl.semaphore_signal(barrier, inc=1, device_id={"expert": mate}, device_id_type=MESH)

    @pl.when(z > 0)
    def _():
        pl.semaphore_signal(barrier, inc=1, device_id={"expert": e - 2}, device_id_type=MESH)

    @pl.when(z < chips - 1)
    def _():
        pl.semaphore_signal(barrier, inc=1, device_id={"expert": e + 2}, device_id_type=MESH)

    mine = pl.ds(pl.multiple_of(c * rows, rows), rows)
    tok = x_buf.at[z, d, mine]
    tok_load = pltpu.make_async_copy(tok_hbm, tok, i_sem.at[0])
    ids_load = pltpu.make_async_copy(ids_hbm, ids, i_sem.at[1])
    levels_load = pltpu.make_async_copy(levels_hbm, levels, i_sem.at[2])
    for load in (tok_load, ids_load, levels_load):
        load.start()
    loads = []
    for x in range(exp_dev):
        for i, (source, held) in enumerate(((gate_hbm, gate_w), (up_hbm, up_w))):
            loads.append(pltpu.make_async_copy(source.at[x], held.at[x], w_sem.at[x, i]))
    for x in range(exp_dev):
        loads.append(pltpu.make_async_copy(down_hbm.at[x], down_w.at[x], w_sem.at[x, 2]))
    for load in loads:
        load.start()

    pl.semaphore_wait(barrier, 2 + jnp.minimum(z, 1) + jnp.minimum(chips - 1 - z, 1))

    tok_load.wait()

    def unit(q, core, j):
        at = pl.ds(pl.multiple_of(core * rows, rows), rows)
        if isinstance(j, int) and j == 2:
            return s_buf.at[q, at]
        return x_buf.at[q, j, at]

    def swap():
        return pltpu.make_async_remote_copy(
            src_ref=tok, dst_ref=unit(z, c, d), send_sem=t_send, recv_sem=x_recv.at[z, c, d],
            device_id={"dp": 1 - d}, device_id_type=MESH,
        )

    def forward(q, j, way):
        target = (mate, e + 2, e - 2)[way]
        return pltpu.make_async_remote_copy(
            src_ref=unit(q, c, j), dst_ref=unit(q, c, j),
            send_sem=x_send.at[q, j, way], recv_sem=x_recv.at[q, c, j],
            device_id={"expert": target}, device_id_type=MESH,
        )

    def arrived(q, core, j):
        pltpu.make_async_remote_copy(
            src_ref=unit(q, core, j), dst_ref=unit(q, core, j),
            send_sem=t_send, recv_sem=x_recv.at[q, core, j],
            device_id={"expert": mate}, device_id_type=MESH,
        ).wait_recv()

    def send_own(j, finish=False):
        for way, there in ((0, None), (1, z < chips - 1), (2, z > 0)):
            def go(way=way):
                copy = forward(z, j, way)
                copy.wait_send() if finish else copy.start()
            go() if there is None else pl.when(there)(go)

    def relay(step, finish=False):
        for way in (1, 2):
            q = z - step if way == 1 else z + step
            inside = z >= step if way == 1 else z + step < chips
            further = jnp.logical_and(inside, z < chips - 1) if way == 1 else jnp.logical_and(inside, z > 0)
            for j in (0, 1, 2):
                @pl.when(inside)
                def _(q=q, j=j):
                    if finish:
                        forward(q, j, 0).wait_send()
                    else:
                        arrived(q, c, j)

                @pl.when(further)
                def _(q=q, j=j, way=way):
                    copy = forward(q, j, way)
                    copy.wait_send() if finish else copy.start()

                if not finish:
                    @pl.when(inside)
                    def _(q=q, j=j):
                        forward(q, j, 0).start()

    swap().start()
    send_own(d)
    ids_load.wait()
    levels_load.wait()
    label = lax.broadcasted_iota(jnp.int32, (128, rows), 0)
    share = jnp.zeros((128, rows), jnp.float32)
    for k in range(ids.shape[0]):
        level = levels[k : k + 1, :].astype(jnp.float32) / 256.0
        share = share + jnp.where(ids[k : k + 1, :] == label, level, 0.0)
    s_buf[z, mine, :] = share.T.astype(s_buf.dtype)
    send_own(2)
    arrived(z, c, 1 - d)
    send_own(1 - d)

    table = visit_order(chips)
    order = []
    for step in range(chips):
        q = jnp.int32(0)
        for place in range(chips):
            q = jnp.where(z == place, jnp.int32(table[place][step]), q)
        order.append(q)

    def piece_of(step, x, side, t):
        return hid.at[step, x, side, :, pl.ds(pl.multiple_of(t * WIDE, WIDE), WIDE)]

    def cross(step, x, t):
        return pltpu.make_async_remote_copy(
            src_ref=piece_of(step, x, d, t), dst_ref=piece_of(step, x, d, t),
            send_sem=h_send.at[step, x, t], recv_sem=h_recv.at[step, x, t],
            device_id={"dp": 1 - d}, device_id_type=MESH,
        )

    def crossed(step, x, t):
        pltpu.make_async_remote_copy(
            src_ref=piece_of(step, x, 1 - d, t), dst_ref=piece_of(step, x, 1 - d, t),
            send_sem=h_send.at[step, x, t], recv_sem=h_recv.at[step, x, t],
            device_id={"dp": 1 - d}, device_id_type=MESH,
        ).wait_recv()

    def units(step):
        q = order[step]
        for j in (0, 1, 2):
            arrived(q, 1 - c, j)
        for x in range(exp_dev):
            if step == 0:
                loads[2 * x].wait()
                loads[2 * x + 1].wait()

            @pl.loop(0, ff // WIDE)
            def _(t):
                cols = pl.ds(pl.multiple_of(t * WIDE, WIDE), WIDE)
                low, high = x_buf[q, 0], x_buf[q, 1]
                gate = jnp.dot(low, gate_w[x, :half, cols], preferred_element_type=jnp.float32)
                gate = gate + jnp.dot(high, gate_w[x, half:, cols], preferred_element_type=jnp.float32)
                up = jnp.dot(low, up_w[x, :half, cols], preferred_element_type=jnp.float32)
                up = up + jnp.dot(high, up_w[x, half:, cols], preferred_element_type=jnp.float32)
                hid[step, x, d, :, cols] = (gate / (1.0 + jnp.exp(-gate)) * up).astype(hid.dtype)
                cross(step, x, t).start()


    def hand_over(step, t):
        return pltpu.make_async_remote_copy(
            src_ref=pair_out.at[step, t], dst_ref=pair_in.at[step, t],
            send_sem=p_send.at[step, t], recv_sem=p_recv.at[step, t],
            device_id={"expert": mate}, device_id_type=MESH,
        )

    def give_back(step, t):
        return pltpu.make_async_remote_copy(
            src_ref=ret_out.at[step, t], dst_ref=ret_in.at[z, t],
            send_sem=r_send.at[step, t], recv_sem=r_recv.at[z, t],
            device_id={"expert": order[step] * 2 + c}, device_id_type=MESH,
        )

    def outputs(step):
        q = order[step]
        lanes = lax.broadcasted_iota(jnp.int32, (2 * rows, 128), 1)
        for x in range(exp_dev):
            if step == 0:
                loads[2 * exp_dev + x].wait()
            picked = jnp.where(lanes == e * exp_dev + x, s_buf[q].astype(jnp.float32), 0.0)
            weight = jnp.sum(picked, axis=1, keepdims=True)
            for t in range(ff // WIDE):
                crossed(step, x, t)

            @pl.loop(0, width // WIDE)
            def _(t):
                cols = pl.ds(pl.multiple_of(t * WIDE, WIDE), WIDE)
                res = jnp.dot(hid[step, x, 0], down_w[x, :ff, cols], preferred_element_type=jnp.float32)
                res = res + jnp.dot(hid[step, x, 1], down_w[x, ff:, cols], preferred_element_type=jnp.float32)
                res = res * weight
                for core in range(2):
                    piece = res[core * rows : (core + 1) * rows]
                    if x == 0:
                        part[t, core] = piece
                    else:
                        part[t, core] += piece
                if x == exp_dev - 1:
                    pair_out[step, t] = part[t, 1 - c].astype(pair_out.dtype)
                    hand_over(step, t).start()

        for t in range(width // WIDE):
            hand_over(step, t).wait_recv()
            both = part[t, c] + pair_in[step, t].astype(jnp.float32)
            if step == 0:
                total[t] = both
            else:
                ret_out[step, t] = both.astype(ret_out.dtype)
                give_back(step, t).start()

    relayed = 0
    for step in range(chips):
        needed = max(abs(table[place][step] - place) for place in range(chips))
        while relayed < needed:
            relayed += 1
            relay(relayed)
        units(step)
        if step >= 1:
            if relayed + 1 < chips - 1:
                relayed += 1
                relay(relayed)
            outputs(step - 1)
    outputs(chips - 1)

    for i in range(1, chips):
        q = lax.rem(z + i, chips)
        for t in range(width // WIDE):
            pltpu.make_async_remote_copy(
                src_ref=ret_in.at[q, t], dst_ref=ret_in.at[q, t],
                send_sem=r_send.at[i, t], recv_sem=r_recv.at[q, t],
                device_id={"expert": mate}, device_id_type=MESH,
            ).wait_recv()
    for t in range(width // WIDE):
        full = total[t]
        for i in range(1, chips):
            full = full + ret_in[lax.rem(z + i, chips), t].astype(jnp.float32)
        out[:, t * WIDE : (t + 1) * WIDE] = full.astype(out.dtype)

    swap().wait_send()
    for j in (0, 1, 2):
        send_own(j, finish=True)
    for step in range(1, chips):
        relay(step, finish=True)
        for t in range(width // WIDE):
            give_back(step, t).wait_send()
    for step in range(chips):
        for t in range(width // WIDE):
            hand_over(step, t).wait_send()
        for x in range(exp_dev):
            for t in range(ff // WIDE):
                cross(step, x, t).wait_send()


def dense_on_device(tokens, expert_ids, gate_levels, gate_weight, up_weight, down_weight):
    chips = lax.axis_size("expert") // 2
    rows, own = tokens.shape
    exp_dev, depth, ff = gate_weight.shape
    width = down_weight.shape[2]
    kind = tokens.dtype
    tiles = width // WIDE
    picks = expert_ids.shape[1]
    vmem = pl.BlockSpec(memory_space=pltpu.VMEM)
    anywhere = pl.BlockSpec(memory_space=pl.ANY)
    dma = pltpu.SemaphoreType.DMA
    flops = 2 * chips * 2 * rows * exp_dev * (2 * depth * ff + 2 * ff * width)
    return pl.pallas_call(
        functools.partial(dense_kernel, chips),
        out_shape=jax.ShapeDtypeStruct((rows, width), kind),
        in_specs=[anywhere] * 6,
        out_specs=vmem,
        scratch_shapes=[
            pltpu.VMEM((picks, rows), jnp.int32),
            pltpu.VMEM((picks, rows), jnp.int32),
            pltpu.VMEM(gate_weight.shape, kind),
            pltpu.VMEM(up_weight.shape, kind),
            pltpu.VMEM(down_weight.shape, kind),
            pltpu.VMEM((chips, 2, 2 * rows, own), kind),
            pltpu.VMEM((chips, 2 * rows, 128), kind),
            pltpu.VMEM((chips, exp_dev, 2, 2 * rows, ff), kind),
            pltpu.VMEM((tiles, 2, rows, WIDE), jnp.float32),
            pltpu.VMEM((chips, tiles, rows, WIDE), kind),
            pltpu.VMEM((chips, tiles, rows, WIDE), kind),
            pltpu.VMEM((chips, tiles, rows, WIDE), kind),
            pltpu.VMEM((chips, tiles, rows, WIDE), kind),
            pltpu.VMEM((tiles, rows, WIDE), jnp.float32),
            dma((3,)),
            dma((exp_dev, 3)),
            dma((chips, 3, 3)),
            dma((chips, 2, 3)),
            dma,
            dma((chips, exp_dev, ff // WIDE)),
            dma((chips, exp_dev, ff // WIDE)),
            dma((chips, tiles)),
            dma((chips, tiles)),
            dma((chips, tiles)),
            dma((chips, tiles)),
        ],
        compiler_params=pltpu.CompilerParams(
            collective_id=0, has_side_effects=True, vmem_limit_bytes=67043328
        ),
        cost_estimate=pl.CostEstimate(
            flops=flops, bytes_accessed=2 * 3 * gate_weight.size, transcendentals=0
        ),
    )(tokens, expert_ids.T, gate_levels.T, gate_weight, up_weight, down_weight)


def on_device(tokens, expert_ids, gate_levels, gate_weight, up_weight, down_weight):
    rows, own = tokens.shape
    exp_dev, depth, ff = gate_weight.shape
    n_expert = lax.axis_size("expert")
    width = down_weight.shape[2]
    experts = exp_dev * n_expert
    dense = (
        2 * rows * expert_ids.shape[1] >= rows * experts
        and lax.axis_size("dp") == 2
        and n_expert % 2 == 0
        and n_expert >= 6
        and experts <= 128
        and rows % 16 == 0
        and own % 128 == 0
        and ff % WIDE == 0
        and width % WIDE == 0
    )
    call = dense_on_device if dense else routed_on_device
    return call(tokens, expert_ids, gate_levels, gate_weight, up_weight, down_weight)


def solution(mesh):
    in_specs = (
        P(("groups", "expert"), "dp"),
        P(("groups", "expert"), None),
        P(("groups", "expert"), None),
        P("expert", None, "dp"),
        P("expert", None, "dp"),
        P("expert", None, "dp"),
    )
    out_specs = P(("groups", "expert"), "dp")
    return jax.shard_map(
        on_device, mesh=mesh, in_specs=in_specs, out_specs=out_specs, check_vma=False
    )
```

profile of v0, /device:TPU:0, one launch (start us, length us, event | category | flops | bytes accessed | tf_op | source)
XLA Modules:
  0.0 56.8 jit_solution(3683385169000640932)
XLA Ops:
  0.0 55.2 %shard_map.64 = bf16[64,1024]{1,0:T(8,128)(2,1)} custom-call(bf16[64,1024]{1,0:T(8,128)(2,1)} %tok_hbm.1, s32[8,64]{1,0:T(8,128)} %bitcast.2, s32[8,64]{1,0:T(8,128)} %bitcast.3, bf16[2,2048,768]{2,1,0:T(8,128)(2,1)} %gate_hbm.1, bf16[2,2048,768]{2,1,0:T(8,128)(2,1)} %up_hbm.1, bf16[2,1536,1024]{2,1,0:T(8,128)(2,1)} %down_hbm.1), custom_call_target="tpu_custom_call" | custom-call | flops 9663676416 | bytes 18874368 | tf_op jit(solution)/shard_map/pallas_call | solution.py:350
  55.2 1.6 %copy.8 = bf16[64,1024]{1,0:T(8,128)(2,1)} copy(bf16[64,1024]{1,0:T(8,128)(2,1)} %shard_map.64) | data formatting | bytes 262144
where the time goes:
time: 57.6 us; the launch traced here: 56.8 us
  Pallas kernels  55.2 us (96%)
  local copies, waits for them, and re-layouts  1.57 us (3%)
    pallas_call x1, Pallas kernels, dense_on_device(): pl.pallas_call(functools.partial(dense_kernel, chips), out_shape=jax.Shap...  55.2 us
    unnamed x1, local copies, waits for them, and re-layouts  1.57 us

commit v1 on v0

v1 whole, which is shorter than its diff:
```python
import functools

import jax
import jax.numpy as jnp
from jax import lax
from jax.experimental import pallas as pl
from jax.experimental.pallas import tpu as pltpu
from jax.sharding import PartitionSpec as P

MESH = pl.DeviceIdType.MESH
WIDE = 256


def slot_numbers(chosen_ids, experts, capacity):
    flat_ids = chosen_ids.reshape(-1)
    labels = jnp.arange(experts, dtype=jnp.int32)
    onehot = (flat_ids[:, None] == labels[None, :]).astype(jnp.int32)
    before = jnp.cumsum(onehot, axis=0) - onehot
    position = jnp.sum(before * onehot, axis=1)
    return (flat_ids * capacity + position).reshape(chosen_ids.shape)


def route_matrix(slots, count):
    targets = jnp.arange(count, dtype=jnp.int32)
    return jnp.any(targets[:, None, None] == slots[None, :, :], axis=2).astype(jnp.bfloat16)


def routed_on_device(tokens, expert_ids, gate_levels, gate_weight, up_weight, down_weight):
    tok_dev = tokens.shape[0]
    picks = expert_ids.shape[1]
    exp_dev = gate_weight.shape[0]
    n_expert = lax.axis_size("expert")
    experts = exp_dev * n_expert
    capacity = min(tok_dev, max(2, 2 * tok_dev * picks // experts))
    slot_count = experts * capacity
    own_slots = slot_numbers(expert_ids, experts, capacity)
    route = route_matrix(own_slots, slot_count)
    whole = lax.all_gather(tokens, "dp", axis=1, tiled=True)
    outgoing = jnp.dot(route, whole, preferred_element_type=jnp.float32).astype(jnp.bfloat16)
    outgoing = outgoing.reshape(n_expert, exp_dev, capacity, whole.shape[1])
    arrived = lax.all_to_all(outgoing, "expert", split_axis=0, concat_axis=0, tiled=True)
    gate_part = jnp.einsum(
        "sxcd,xdf->sxcf", arrived, gate_weight, preferred_element_type=jnp.float32
    )
    up_part = jnp.einsum("sxcd,xdf->sxcf", arrived, up_weight, preferred_element_type=jnp.float32)
    hidden = (jax.nn.silu(gate_part) * up_part).astype(jnp.bfloat16)
    out_features = down_weight.shape[2]
    outputs = jnp.einsum(
        "sxcf,xfk->sxck",
        lax.all_gather(hidden, "dp", axis=3, tiled=True),
        down_weight,
        preferred_element_type=jnp.float32,
    )
    result = outputs.astype(jnp.bfloat16)
    returned = lax.all_to_all(result, "expert", split_axis=0, concat_axis=0, tiled=True)
    returned = returned.reshape(slot_count, out_features)
    shares = gate_levels.astype(jnp.float32) / 256.0
    targets = jnp.arange(slot_count, dtype=jnp.int32)
    weighting = jnp.sum(
        jnp.where(
            targets[None, :, None] == own_slots[:, None, :], shares[:, None, :], jnp.float32(0.0)
        ),
        axis=2,
    )
    weighting = weighting.astype(jnp.bfloat16)
    combined = jnp.dot(weighting, returned, preferred_element_type=jnp.float32)
    return combined.astype(jnp.bfloat16)


def visit_order(chips):
    return [
        sorted(range(chips), key=lambda q: (abs(q - z), q if 2 * z < chips else -q)) for z in range(chips)
    ]


def crossings(chips, exp_dev, rows):
    piece, late = rows // 2, exp_dev - 1
    parts = [(0, "own", 0, piece, 0), (0, "own", piece, piece, 0), (0, "own", 0, piece, late), (0, "mate", 0, rows, 0)]
    for role in range(1, chips):
        for x in range(late):
            parts.append((role, "all", 0, 2 * rows, x))
        if role < 3:
            parts.append((role, "all", 0, rows, late))
            parts.append((role, "all", rows, rows, late))
        else:
            parts.append((role, "all", 0, 2 * rows, late))
    for x in range(1, exp_dev):
        parts.append((0, "mate", 0, rows, x))
    for x in range(1, late):
        parts.append((0, "own", 0, rows, x))
    parts.append((0, "own", piece, piece, late))
    return parts


def dense_kernel(
    chips, tok_hbm, ids_hbm, levels_hbm, gate_hbm, up_hbm, down_hbm, out,
    ids, levels, gate_w, up_w, down_w, x_buf, hid, acc, pair_out, pair_in, ret_out, ret_in,
    i_sem, w_sem, x_send, x_recv, c_recv, m_recv, t_send, n_send, h_send, h_recv, p_send, p_recv, r_send, r_recv,
):
    e = lax.axis_index("expert")
    d = lax.axis_index("dp")
    z, c = lax.div(e, 2), lax.rem(e, 2)
    rows, own = tok_hbm.shape
    exp_dev, depth, ff = gate_w.shape
    width = down_w.shape[2]
    tiles = width // WIDE
    piece = rows // 2
    mate = z * 2 + 1 - c

    barrier = pltpu.get_barrier_semaphore()
    pl.semaphore_signal(barrier, inc=1, device_id={"dp": 1 - d}, device_id_type=MESH)
    pl.semaphore_signal(barrier, inc=1, device_id={"expert": mate}, device_id_type=MESH)

    @pl.when(z > 0)
    def _():
        pl.semaphore_signal(barrier, inc=1, device_id={"expert": e - 2}, device_id_type=MESH)

    @pl.when(z < chips - 1)
    def _():
        pl.semaphore_signal(barrier, inc=1, device_id={"expert": e + 2}, device_id_type=MESH)

    def block(core):
        return pl.ds(pl.multiple_of(core * rows, rows), rows)

    def unit(q, core, j, h):
        at = pl.ds(pl.multiple_of(core * rows + h * piece, piece), piece)
        return x_buf.at[q, at, pl.ds(pl.multiple_of(j * own, own), own)]

    tok_loads = []
    for h in range(2):
        source = tok_hbm.at[pl.ds(h * piece, piece)]
        tok_loads.append(pltpu.make_async_copy(source, unit(z, c, d, h), i_sem.at[2 + h]))
    ids_load = pltpu.make_async_copy(ids_hbm, ids, i_sem.at[0])
    levels_load = pltpu.make_async_copy(levels_hbm, levels, i_sem.at[1])
    for load in (*tok_loads, ids_load, levels_load):
        load.start()
    loads = {}
    for x in range(exp_dev):
        for i, (source, held) in enumerate(((gate_hbm, gate_w), (up_hbm, up_w))):
            loads[i, x] = pltpu.make_async_copy(source.at[x], held.at[x], w_sem.at[x, i])
    for x in range(exp_dev):
        loads[2, x] = pltpu.make_async_copy(down_hbm.at[x], down_w.at[x], w_sem.at[x, 2])
    for load in tok_loads:
        load.wait()
    for load in loads.values():
        load.start()
    pending = set(loads)

    def loaded(*keys):
        for key in keys:
            if key in pending:
                pending.remove(key)
                loads[key].wait()

    pl.semaphore_wait(barrier, 2 + jnp.minimum(z, 1) + jnp.minimum(chips - 1 - z, 1))

    shares = pl.ds(depth, 128)

    def swap(h):
        return pltpu.make_async_remote_copy(
            src_ref=unit(z, c, d, h), dst_ref=unit(z, c, d, h),
            send_sem=n_send, recv_sem=x_recv.at[z, d, h],
            device_id={"dp": 1 - d}, device_id_type=MESH,
        )

    def push(ref, q, way, sem):
        return pltpu.make_async_remote_copy(
            src_ref=ref, dst_ref=ref, send_sem=x_send.at[q, way], recv_sem=m_recv.at[q] if way == 0 else sem,
            device_id={"expert": (mate, e + 2, e - 2)[way]}, device_id_type=MESH,
        )

    def forward(q, j, h, way):
        return push(unit(q, c, j, h), q, way, x_recv.at[q, j, h])

    def forward_share(q, way):
        return push(x_buf.at[q, block(c), shares], q, way, c_recv.at[q])

    def await_copy(ref, sem, sent=False):
        copy = pltpu.make_async_remote_copy(
            src_ref=ref, dst_ref=ref, send_sem=sem if sent else t_send, recv_sem=t_send if sent else sem,
            device_id={"expert": mate}, device_id_type=MESH,
        )
        copy.wait_send() if sent else copy.wait_recv()

    def arrived(q, j, h):
        await_copy(unit(q, c, j, h), x_recv.at[q, j, h])

    def send_all(make):
        pl.when(z < chips - 1)(lambda: make(1).start())
        pl.when(z > 0)(lambda: make(2).start())
        make(0).start()

    def send_own(j, h):
        send_all(lambda way: forward(z, j, h, way))

    def pass_on(step, make, wait):
        for way in (1, 2):
            q = z - step if way == 1 else z + step
            inside = z >= step if way == 1 else z + step < chips
            further = jnp.logical_and(inside, z < chips - 1) if way == 1 else jnp.logical_and(inside, z > 0)

            @pl.when(inside)
            def _(q=q):
                wait(q)
                make(q, 0).start()

            @pl.when(further)
            def _(q=q, way=way):
                make(q, way).start()

    def relay(step, j, h):
        pass_on(step, lambda q, way: forward(q, j, h, way), lambda q: arrived(q, j, h))

    def relay_share(step):
        pass_on(step, forward_share, lambda q: await_copy(x_buf.at[q, block(c), shares], c_recv.at[q]))

    for h in range(2):
        swap(h).start()
    for h in range(2):
        send_own(d, h)
    ids_load.wait()
    levels_load.wait()
    label = lax.broadcasted_iota(jnp.int32, (128, rows), 0)
    share = jnp.zeros((128, rows), jnp.float32)
    for k in range(ids.shape[0]):
        level = levels[k : k + 1, :].astype(jnp.float32) / 256.0
        share = share + jnp.where(ids[k : k + 1, :] == label, level, 0.0)
    x_buf[z, block(c), shares] = share.T.astype(x_buf.dtype)
    send_all(lambda way: forward_share(z, way))

    table = visit_order(chips)
    order = []
    for step in range(chips):
        q = jnp.int32(0)
        for place in range(chips):
            q = jnp.where(z == place, jnp.int32(table[place][step]), q)
        order.append(q)

    def row_range(kind, start, size):
        if kind == "all":
            return pl.ds(start, size)
        core = c if kind == "own" else 1 - c
        return pl.ds(pl.multiple_of(core * rows + start, piece), size)

    items = crossings(chips, exp_dev, rows)
    spot = {item: i for i, item in enumerate(items)}

    def piece_of(i, side, t):
        role, kind, start, size, x = items[i]
        cols = pl.ds(pl.multiple_of(side * ff + t * WIDE, WIDE), WIDE)
        return hid.at[role, x, row_range(kind, start, size), cols]

    def cross(i, t):
        return pltpu.make_async_remote_copy(
            src_ref=piece_of(i, d, t), dst_ref=piece_of(i, d, t),
            send_sem=h_send, recv_sem=h_recv.at[i],
            device_id={"dp": 1 - d}, device_id_type=MESH,
        )

    def crossed(i):
        role, kind, start, size, x = items[i]
        cols = pl.ds(pl.multiple_of((1 - d) * ff, WIDE), ff)
        await_copy(hid.at[role, x, row_range(kind, start, size), cols], h_recv.at[i])

    seen = set()
    met = set()


    def enter(role, kind, x):
        if kind != "own" and role not in seen:
            seen.add(role)
            await_copy(x_buf.at[order[role], block(1 - c)], m_recv.at[order[role]])
        loaded((0, x), (1, x))

    def release(*chosen):
        for i in chosen:
            for t in range(ff // WIDE):
                cross(i, t).start()

    def units(role, kind, start, size, x, now=(), then=()):
        enter(role, kind, x)
        at = row_range(kind, start, size)

        def finish(t, gate, up):
            put = pl.ds(pl.multiple_of(d * ff + t * WIDE, WIDE), WIDE)
            hid[role, x, at, put] = (gate / (1.0 + jnp.exp(-gate)) * up).astype(hid.dtype)
            for i in now:
                cross(i, t).start()

        held = None
        for t in range(ff // WIDE):
            cols = slice(t * WIDE, (t + 1) * WIDE)
            lhs = x_buf[order[role], at, :depth]
            gate = jnp.dot(lhs, gate_w[x, :, cols], preferred_element_type=jnp.float32)
            up = jnp.dot(lhs, up_w[x, :, cols], preferred_element_type=jnp.float32)
            if held is not None:
                finish(*held)
            held = (t, gate, up)
        finish(*held)
        release(*then)

    def hand_over(role, t):
        return pltpu.make_async_remote_copy(
            src_ref=pair_out.at[role, t], dst_ref=pair_in.at[role, t],
            send_sem=p_send, recv_sem=p_recv.at[role, t],
            device_id={"expert": mate}, device_id_type=MESH,
        )

    def give_back(role, t):
        return pltpu.make_async_remote_copy(
            src_ref=ret_out.at[role, t], dst_ref=ret_in.at[z, t],
            send_sem=r_send, recv_sem=r_recv,
            device_id={"expert": order[role] * 2 + c}, device_id_type=MESH,
        )

    def share_of(role, at, size, x):
        lanes = lax.broadcasted_iota(jnp.int32, (size, 128), 1)
        picked = jnp.where(lanes == e * exp_dev + x, x_buf[order[role], at, shares].astype(jnp.float32), 0.0)
        return jnp.sum(picked, axis=1, keepdims=True)

    def outputs(role, kind, start, size, x, side=None, first=False, last=False, turn=None):
        at = row_range(kind, start, size)
        loaded((2, x))
        weight = share_of(role, at, size, x)
        if side != "own":
            for i, (a, b, begin, count, y) in enumerate(items):
                if (a, b, y) == (role, kind, x) and begin < start + size and start < begin + count and i not in met:
                    met.add(i)
                    crossed(i)
        if side is None:
            depth_at = slice(0, 2 * ff)
        else:
            depth_at = pl.ds(pl.multiple_of((d if side == "own" else 1 - d) * ff, WIDE), ff)

        def put(t, res):
            cols = slice(t * WIDE, (t + 1) * WIDE)
            res = res * weight
            if not first:
                res = res + acc[role, at, cols]
            if not last:
                acc[role, at, cols] = res
                return
            if kind == "mate":
                pair_out[role, t] = res.astype(pair_out.dtype)
                hand_over(role, t).start()
            elif turn is None:
                acc[role, at, cols] = res
                pair_out[role, t] = acc[role, block(1 - c), cols].astype(pair_out.dtype)
                hand_over(role, t).start()
            else:
                acc[role, at, cols] = res
                slot = jnp.where(c == turn, chips, role)
                pair_out[slot, t] = res.astype(pair_out.dtype)

                @pl.when(c != turn)
                def _():
                    hand_over(role, t).start()

        held = None
        for t in range(tiles):
            cols = slice(t * WIDE, (t + 1) * WIDE)
            res = jnp.dot(hid[role, x, at, depth_at], down_w[x, depth_at, cols], preferred_element_type=jnp.float32)
            if held is not None:
                put(*held)
            held = (t, res)
        put(*held)

    def combine(role, turn=None):
        def go():
            for t in range(tiles):
                cols = slice(t * WIDE, (t + 1) * WIDE)
                hand_over(role, t).wait_recv()
                both = acc[role, block(c), cols] + pair_in[role, t].astype(jnp.float32)
                ret_out[role, t] = both.astype(ret_out.dtype)
                give_back(role, t).start()

        go() if turn is None else pl.when(c == turn)(go)

    late = exp_dev - 1
    far = chips - 1

    def remote(role, x):
        now = then = ()
        if x < late:
            now = (spot[role, "all", 0, 2 * rows, x],)
        elif role == 1:
            now = (spot[role, "all", 0, rows, x],)
        elif role > 2:
            now = (spot[role, "all", 0, 2 * rows, x],)
        units(role, "all", 0, 2 * rows, x, now=now)

    def bulk(role):
        for x in range(late):
            outputs(role, "all", 0, 2 * rows, x, first=x == 0)

    arrived(z, 1 - d, 0)
    send_own(1 - d, 0)
    units(0, "own", 0, piece, 0, now=(0,))
    arrived(z, 1 - d, 1)
    send_own(1 - d, 1)
    units(0, "own", piece, piece, 0, now=(1,))
    relay(1, d, 0)
    relay(1, d, 1)
    units(0, "own", 0, rows, late, now=(2,))
    relay_share(1)
    relay(1, 1 - d, 0)
    units(0, "mate", 0, rows, 0, now=(3,))
    relay(1, 1 - d, 1)
    for x in range(1, late):
        units(0, "own", 0, rows, x)

    for step in range(1, chips):
        more = step + 1 < chips
        for x in range(late):
            remote(step, x)
        if more:
            relay(step + 1, d, 0)
            relay(step + 1, d, 1)
        if step == 1:
            outputs(0, "own", 0, rows, 0, first=True)
        if more:
            relay(step + 1, 1 - d, 0)
        remote(step, late)
        if more:
            relay_share(step + 1)
        if step == 1:
            outputs(0, "mate", 0, rows, 0, first=True)
        if more:
            relay(step + 1, 1 - d, 1)
        if step == 2:
            bulk(1)
            outputs(1, "all", 0, rows, late, last=True, turn=0)
        if step == 3:
            combine(1, 0)
        if step == 4:
            bulk(2)
        if step > 4:
            bulk(step - 2)
            outputs(step - 2, "all", 0, 2 * rows, late, last=True)
            combine(step - 2)
    release(spot[2, "all", 0, rows, late], spot[2, "all", rows, rows, late], spot[1, "all", rows, rows, late])
    for x in range(1, exp_dev):
        units(0, "mate", 0, rows, x, now=(spot[0, "mate", 0, rows, x],))
    release(*(spot[0, "own", 0, rows, x] for x in range(1, late)), spot[0, "own", piece, piece, late])
    if chips == 3:
        combine(1, 0)
    if chips < 5:
        bulk(2)
    if chips > 4:
        bulk(far - 1)
        outputs(far - 1, "all", 0, 2 * rows, late, last=True)
        combine(far - 1)
    if far > 2:
        bulk(far)
        outputs(far, "all", 0, 2 * rows, late, last=True)
    outputs(2, "all", 0, 2 * rows, late, side="own")
    outputs(1, "all", rows, rows, late, side="own")
    if far > 2:
        combine(far)
    for x in range(1, exp_dev):
        outputs(0, "mate", 0, rows, x, side="own")
        outputs(0, "own", 0, rows, x, side="own")
    for turn in range(2):
        outputs(2, "all", turn * rows, rows, late, side="other", last=True, turn=turn)
    for turn in range(2):
        combine(2, turn)
    outputs(1, "all", rows, rows, late, side="other", last=True, turn=1)
    for x in range(1, late):
        outputs(0, "mate", 0, rows, x, side="other")
    combine(1, 1)
    outputs(0, "mate", 0, rows, late, side="other", last=True)
    for x in range(1, exp_dev):
        outputs(0, "own", 0, rows, x, side="other")

    for t in range(tiles):
        hand_over(0, t).wait_recv()
    await_copy(ret_in.at[pl.ds(0, chips - 1)], r_recv)
    for t in range(tiles):
        cols = slice(t * WIDE, (t + 1) * WIDE)
        full = acc[0, block(c), cols] + pair_in[0, t].astype(jnp.float32)
        for i in range(1, chips):
            full = full + ret_in[lax.rem(z + i, chips), t].astype(jnp.float32)
        out[:, cols] = full.astype(out.dtype)

    await_copy(x_buf.at[z, block(c), pl.ds(pl.multiple_of(d * own, own), own)], n_send, sent=True)
    for q in range(chips):
        await_copy(x_buf.at[q, block(c)], x_send.at[q, 0], sent=True)
        for way, sends in ((1, jnp.logical_and(q <= z, z < chips - 1)), (2, jnp.logical_and(q >= z, z > 0))):
            @pl.when(sends)
            def _(q=q, way=way):
                await_copy(x_buf.at[q, block(c)], x_send.at[q, way], sent=True)
    await_copy(hid.at[:, :, :, pl.ds(pl.multiple_of(d * ff, WIDE), ff)], h_send, sent=True)
    await_copy(pair_out.at[pl.ds(0, chips)], p_send, sent=True)
    await_copy(ret_out.at[pl.ds(1, chips - 1)], r_send, sent=True)


def dense_on_device(tokens, expert_ids, gate_levels, gate_weight, up_weight, down_weight):
    chips = lax.axis_size("expert") // 2
    rows, own = tokens.shape
    exp_dev, depth, ff = gate_weight.shape
    width = down_weight.shape[2]
    kind = tokens.dtype
    tiles = width // WIDE
    picks = expert_ids.shape[1]
    count = len(crossings(chips, exp_dev, rows))
    anywhere = pl.BlockSpec(memory_space=pl.ANY)
    dma = pltpu.SemaphoreType.DMA
    operands = [
        pltpu.with_memory_space_constraint(a, memory_space=pltpu.HBM)
        for a in (tokens, expert_ids.T, gate_levels.T, gate_weight, up_weight, down_weight)
    ]
    flops = 2 * chips * 2 * rows * exp_dev * (2 * depth * ff + 2 * ff * width)
    return pl.pallas_call(
        functools.partial(dense_kernel, chips),
        out_shape=jax.ShapeDtypeStruct((rows, width), kind),
        in_specs=[anywhere] * 6,
        out_specs=pl.BlockSpec(memory_space=pltpu.VMEM),
        scratch_shapes=[
            pltpu.VMEM((picks, rows), jnp.int32),
            pltpu.VMEM((picks, rows), jnp.int32),
            pltpu.VMEM(gate_weight.shape, kind),
            pltpu.VMEM(up_weight.shape, kind),
            pltpu.VMEM(down_weight.shape, kind),
            pltpu.VMEM((chips, 2 * rows, depth + 128), kind),
            pltpu.VMEM((chips, exp_dev, 2 * rows, 2 * ff), kind),
            pltpu.VMEM((chips, 2 * rows, width), jnp.float32),
            pltpu.VMEM((chips + 1, tiles, rows, WIDE), kind),
            pltpu.VMEM((chips, tiles, rows, WIDE), kind),
            pltpu.VMEM((chips, tiles, rows, WIDE), kind),
            pltpu.VMEM((chips, tiles, rows, WIDE), kind),
            dma((4,)),
            dma((exp_dev, 3)),
            dma((chips, 3)),
            dma((chips, 2, 2)),
            dma((chips,)),
            dma((chips,)),
            dma,
            dma,
            dma,
            dma((count,)),
            dma,
            dma((chips, tiles)),
            dma,
            dma,
        ],
        compiler_params=pltpu.CompilerParams(
            collective_id=0, has_side_effects=True, vmem_limit_bytes=50331648
        ),
        cost_estimate=pl.CostEstimate(
            flops=flops, bytes_accessed=2 * 3 * gate_weight.size, transcendentals=0
        ),
    )(*operands)


def on_device(tokens, expert_ids, gate_levels, gate_weight, up_weight, down_weight):
    rows, own = tokens.shape
    exp_dev, depth, ff = gate_weight.shape
    n_expert = lax.axis_size("expert")
    width = down_weight.shape[2]
    experts = exp_dev * n_expert
    dense = (
        2 * rows * expert_ids.shape[1] >= rows * experts
        and lax.axis_size("dp") == 2
        and n_expert % 2 == 0
        and n_expert >= 6
        and experts <= 128
        and rows % 32 == 0
        and exp_dev >= 2
        and own % 128 == 0
        and ff % WIDE == 0
        and width % WIDE == 0
    )
    call = dense_on_device if dense else routed_on_device
    return call(tokens, expert_ids, gate_levels, gate_weight, up_weight, down_weight)


def solution(mesh):
    in_specs = (
        P(("groups", "expert"), "dp"),
        P(("groups", "expert"), None),
        P(("groups", "expert"), None),
        P("expert", None, "dp"),
        P("expert", None, "dp"),
        P("expert", None, "dp"),
    )
    out_specs = P(("groups", "expert"), "dp")
    return jax.shard_map(
        on_device, mesh=mesh, in_specs=in_specs, out_specs=out_specs, check_vma=False
    )
```

time: 57.6 us -> 50.1 us (0.87)
  the two profiles are of different devices: /device:TPU:0 before, /device:TPU:11 now
where the time goes in v1:
time: 50.1 us; the launch traced here: 49.9 us
  Pallas kernels  49.3 us (98%)
  local copies, waits for them, and re-layouts  0.66 us (1%)
    pallas_call x1, Pallas kernels, dense_on_device(): pl.pallas_call(functools.partial(dense_kernel, chips), out_shape=jax.Shap...  49.3 us

profile of v1, /device:TPU:11, one launch (start us, length us, event | category | flops | bytes accessed | tf_op | source)
XLA Modules:
  0.0 49.9 jit_solution(16863604739494994825)
XLA Ops:
  0.0 49.3 %shard_map.64 = bf16[64,1024]{1,0:T(8,128)(2,1)S(1)} custom-call(bf16[64,1024]{1,0:T(8,128)(2,1)} %tok_hbm.1, s32[8,64]{1,0:T(8,128)} %bitcast.2, s32[8,64]{1,0:T(8,128)} %bitcast.3, bf16[2,2048,768]{2,1,0:T(8,128)(2,1)} %gate_hbm.1, bf16[2,2048,768]{2,1,0:T(8,128)(2,1)} %up_hbm.1, bf16[2,1536,1024]{2,1,0:T(8,128)(2,1)} %down_hbm.1), custom_call_target="tpu_custom_call" | custom-call | flops 9663676416 | bytes 18874368 | tf_op jit(solution)/shard_map/pallas_call | solution.py:513
  49.3 0.7 %copy.8 = bf16[64,1024]{1,0:T(8,128)(2,1)} copy(bf16[64,1024]{1,0:T(8,128)(2,1)S(1)} %shard_map.64) | data formatting | bytes 262144

commit v2 on v1

--- a/solution.py
+++ b/solution.py
@@ -68,22 +68,26 @@
 
 
 def visit_order(chips):
-    return [
-        sorted(range(chips), key=lambda q: (abs(q - z), q if 2 * z < chips else -q)) for z in range(chips)
-    ]
+    table = []
+    for z in range(chips):
+        up = 2 * z < chips
+        inward = sorted((q for q in range(chips) if q != z and (q > z) == up), key=lambda q: abs(q - z))
+        outward = sorted((q for q in range(chips) if q != z and (q > z) != up), key=lambda q: -abs(q - z))
+        table.append([z, *inward, *outward])
+    return table
 
 
 def crossings(chips, exp_dev, rows):
     piece, late = rows // 2, exp_dev - 1
     parts = [(0, "own", 0, piece, 0), (0, "own", piece, piece, 0), (0, "own", 0, piece, late), (0, "mate", 0, rows, 0)]
-    for role in range(1, chips):
-        for x in range(late):
-            parts.append((role, "all", 0, 2 * rows, x))
-        if role < 3:
-            parts.append((role, "all", 0, rows, late))
-            parts.append((role, "all", rows, rows, late))
-        else:
-            parts.append((role, "all", 0, 2 * rows, late))
+    for x in range(late):
+        parts.append((1, "all", 0, 2 * rows, x))
+    for turn in range(2):
+        parts.append((1, "all", turn * rows, rows, late))
+    for role in range(2, chips):
+        for turn in range(2):
+            for x in range(exp_dev):
+                parts.append((role, "all", turn * rows, rows, x))
     for x in range(1, exp_dev):
         parts.append((0, "mate", 0, rows, x))
     for x in range(1, late):
@@ -380,18 +384,16 @@
     far = chips - 1
 
     def remote(role, x):
-        now = then = ()
-        if x < late:
-            now = (spot[role, "all", 0, 2 * rows, x],)
-        elif role == 1:
-            now = (spot[role, "all", 0, rows, x],)
-        elif role > 2:
-            now = (spot[role, "all", 0, 2 * rows, x],)
-        units(role, "all", 0, 2 * rows, x, now=now)
-
-    def bulk(role):
-        for x in range(late):
-            outputs(role, "all", 0, 2 * rows, x, first=x == 0)
+        if role == 1 and x < late:
+            units(role, "all", 0, 2 * rows, x, now=(spot[role, "all", 0, 2 * rows, x],))
+            return
+        then = (spot[role, "all", rows, rows, y] for y in range(exp_dev)) if role > 1 and x == late else ()
+        units(role, "all", 0, 2 * rows, x, now=(spot[role, "all", 0, rows, x],), then=then)
+
+    def half(role, turn, side=None):
+        for x in range(exp_dev):
+            first = x == 0 and side is None
+            outputs(role, "all", turn * rows, rows, x, side=side, first=first, last=x == late, turn=turn)
 
     arrived(z, 1 - d, 0)
     send_own(1 - d, 0)
@@ -399,9 +401,9 @@
     arrived(z, 1 - d, 1)
     send_own(1 - d, 1)
     units(0, "own", piece, piece, 0, now=(1,))
+    units(0, "own", 0, rows, late, now=(2,))
     relay(1, d, 0)
     relay(1, d, 1)
-    units(0, "own", 0, rows, late, now=(2,))
     relay_share(1)
     relay(1, 1 - d, 0)
     units(0, "mate", 0, rows, 0, now=(3,))
@@ -413,6 +415,8 @@
         more = step + 1 < chips
         for x in range(late):
             remote(step, x)
+        if step > 1:
+            remote(step, late)
         if more:
             relay(step + 1, d, 0)
             relay(step + 1, d, 1)
@@ -420,50 +424,46 @@
             outputs(0, "own", 0, rows, 0, first=True)
         if more:
             relay(step + 1, 1 - d, 0)
-        remote(step, late)
+        if step == 1:
+            remote(step, late)
         if more:
             relay_share(step + 1)
         if step == 1:
             outputs(0, "mate", 0, rows, 0, first=True)
         if more:
             relay(step + 1, 1 - d, 1)
-        if step == 2:
-            bulk(1)
-            outputs(1, "all", 0, rows, late, last=True, turn=0)
-        if step == 3:
-            combine(1, 0)
-        if step == 4:
-            bulk(2)
-        if step > 4:
-            bulk(step - 2)
-            outputs(step - 2, "all", 0, 2 * rows, late, last=True)
-            combine(step - 2)
-    release(spot[2, "all", 0, rows, late], spot[2, "all", rows, rows, late], spot[1, "all", rows, rows, late])
+        if step > 3:
+            for turn in range(2):
+                half(step - 2, turn)
+            for turn in range(2):
+                combine(step - 2, turn)
+    release(spot[1, "all", rows, rows, late])
     for x in range(1, exp_dev):
         units(0, "mate", 0, rows, x, now=(spot[0, "mate", 0, rows, x],))
     release(*(spot[0, "own", 0, rows, x] for x in range(1, late)), spot[0, "own", piece, piece, late])
-    if chips == 3:
-        combine(1, 0)
-    if chips < 5:
-        bulk(2)
-    if chips > 4:
-        bulk(far - 1)
-        outputs(far - 1, "all", 0, 2 * rows, late, last=True)
-        combine(far - 1)
+    for x in range(late):
+        outputs(1, "all", 0, 2 * rows, x, first=x == 0)
+    outputs(1, "all", 0, rows, late, last=True, turn=0)
     if far > 2:
-        bulk(far)
-        outputs(far, "all", 0, 2 * rows, late, last=True)
-    outputs(2, "all", 0, 2 * rows, late, side="own")
+        half(far - 1, 0)
+    combine(1, 0)
+    if far > 2:
+        combine(far - 1, 0)
+        half(far - 1, 1)
+    for x in range(exp_dev):
+        outputs(far, "all", 0, 2 * rows, x, side="own", first=x == 0)
+    if far > 2:
+        combine(far - 1, 1)
     outputs(1, "all", rows, rows, late, side="own")
-    if far > 2:
-        combine(far)
     for x in range(1, exp_dev):
         outputs(0, "mate", 0, rows, x, side="own")
         outputs(0, "own", 0, rows, x, side="own")
-    for turn in range(2):
-        outputs(2, "all", turn * rows, rows, late, side="other", last=True, turn=turn)
-    for turn in range(2):
-        combine(2, turn)
+    half(far, 0, side="other")
+    for x in range(late):
+        outputs(far, "all", rows, rows, x, side="other")
+    combine(far, 0)
+    outputs(far, "all", rows, rows, late, side="other", last=True, turn=1)
+    combine(far, 1)
     outputs(1, "all", rows, rows, late, side="other", last=True, turn=1)
     for x in range(1, late):
         outputs(0, "mate", 0, rows, x, side="other")

time: 50.1 us -> 47.4 us (0.946)
  the two profiles are of different devices: /device:TPU:11 before, /device:TPU:0 now
where the time goes in v2:
time: 47.4 us; the launch traced here: 46.5 us
  Pallas kernels  45.9 us (97%)
  local copies, waits for them, and re-layouts  0.66 us (1%)
    pallas_call x1, Pallas kernels, dense_on_device(): pl.pallas_call(functools.partial(dense_kernel, chips), out_shape=jax.Shap...  45.9 us

profile of v2, /device:TPU:0, one launch (start us, length us, event | category | flops | bytes accessed | tf_op | source)
XLA Modules:
  0.0 46.5 jit_solution(10967257293117193171)
XLA Ops:
  0.0 45.9 %shard_map.64 = bf16[64,1024]{1,0:T(8,128)(2,1)S(1)} custom-call(bf16[64,1024]{1,0:T(8,128)(2,1)} %tok_hbm.1, s32[8,64]{1,0:T(8,128)} %bitcast.2, s32[8,64]{1,0:T(8,128)} %bitcast.3, bf16[2,2048,768]{2,1,0:T(8,128)(2,1)} %gate_hbm.1, bf16[2,2048,768]{2,1,0:T(8,128)(2,1)} %up_hbm.1, bf16[2,1536,1024]{2,1,0:T(8,128)(2,1)} %down_hbm.1), custom_call_target="tpu_custom_call" | custom-call | flops 9663676416 | bytes 18874368 | tf_op jit(solution)/shard_map/pallas_call | solution.py:513
  45.9 0.7 %copy.8 = bf16[64,1024]{1,0:T(8,128)(2,1)} copy(bf16[64,1024]{1,0:T(8,128)(2,1)S(1)} %shard_map.64) | data formatting | bytes 262144

commit v3 on v2

--- a/solution.py
+++ b/solution.py
@@ -419,15 +419,15 @@
             remote(step, late)
         if more:
             relay(step + 1, d, 0)
+        if step == 1:
+            remote(step, late)
+        if more:
             relay(step + 1, d, 1)
+            relay_share(step + 1)
         if step == 1:
             outputs(0, "own", 0, rows, 0, first=True)
         if more:
             relay(step + 1, 1 - d, 0)
-        if step == 1:
-            remote(step, late)
-        if more:
-            relay_share(step + 1)
         if step == 1:
             outputs(0, "mate", 0, rows, 0, first=True)
         if more:
@@ -448,8 +448,8 @@
         half(far - 1, 0)
     combine(1, 0)
     if far > 2:
+        half(far - 1, 1)
         combine(far - 1, 0)
-        half(far - 1, 1)
     for x in range(exp_dev):
         outputs(far, "all", 0, 2 * rows, x, side="own", first=x == 0)
     if far > 2:

time: 47.4 us -> 46.2 us (0.975); the launches traced: 46.5 us -> 46 us
  Pallas kernels: 45.9 us -> 45.3 us
    pallas_call x1, Pallas kernels: 45.9 us -> 45.3 us  [dense_on_device(): pl.pallas_call(functools.partial(dense_kernel, chips), out_shape=jax.Shap...]
where the time goes in v3:
time: 46.2 us; the launch traced here: 46 us
  Pallas kernels  45.3 us (98%)
  local copies, waits for them, and re-layouts  0.66 us (1%)
    pallas_call x1, Pallas kernels, dense_on_device(): pl.pallas_call(functools.partial(dense_kernel, chips), out_shape=jax.Shap...  45.3 us

profile of v3, /device:TPU:0, one launch (start us, length us, event | category | flops | bytes accessed | tf_op | source)
XLA Modules:
  0.0 46.0 jit_solution(8959512692368651571)
XLA Ops:
  0.0 45.3 %shard_map.64 = bf16[64,1024]{1,0:T(8,128)(2,1)S(1)} custom-call(bf16[64,1024]{1,0:T(8,128)(2,1)} %tok_hbm.1, s32[8,64]{1,0:T(8,128)} %bitcast.2, s32[8,64]{1,0:T(8,128)} %bitcast.3, bf16[2,2048,768]{2,1,0:T(8,128)(2,1)} %gate_hbm.1, bf16[2,2048,768]{2,1,0:T(8,128)(2,1)} %up_hbm.1, bf16[2,1536,1024]{2,1,0:T(8,128)(2,1)} %down_hbm.1), custom_call_target="tpu_custom_call" | custom-call | flops 9663676416 | bytes 18874368 | tf_op jit(solution)/shard_map/pallas_call | solution.py:513
  45.3 0.7 %copy.8 = bf16[64,1024]{1,0:T(8,128)(2,1)} copy(bf16[64,1024]{1,0:T(8,128)(2,1)S(1)} %shard_map.64) | data formatting | bytes 262144

commit v4 on v3

--- a/solution.py
+++ b/solution.py
@@ -81,7 +81,7 @@
     piece, late = rows // 2, exp_dev - 1
     parts = [(0, "own", 0, piece, 0), (0, "own", piece, piece, 0), (0, "own", 0, piece, late), (0, "mate", 0, rows, 0)]
     for x in range(late):
-        parts.append((1, "all", 0, 2 * rows, x))
+        parts += [(1, "own", 0, rows, x), (1, "mate", 0, rows, x)]
     for turn in range(2):
         parts.append((1, "all", turn * rows, rows, late))
     for role in range(2, chips):
@@ -169,7 +169,7 @@
 
     def push(ref, q, way, sem):
         return pltpu.make_async_remote_copy(
-            src_ref=ref, dst_ref=ref, send_sem=x_send.at[q, way], recv_sem=m_recv.at[q] if way == 0 else sem,
+            src_ref=ref, dst_ref=ref, send_sem=x_send.at[way], recv_sem=m_recv.at[q] if way == 0 else sem,
             device_id={"expert": (mate, e + 2, e - 2)[way]}, device_id_type=MESH,
         )
 
@@ -328,7 +328,8 @@
         weight = share_of(role, at, size, x)
         if side != "own":
             for i, (a, b, begin, count, y) in enumerate(items):
-                if (a, b, y) == (role, kind, x) and begin < start + size and start < begin + count and i not in met:
+                same = b == kind and begin < start + size and start < begin + count
+                if (a, y) == (role, x) and (same or (kind == "all" and b != "all")) and i not in met:
                     met.add(i)
                     crossed(i)
         if side is None:
@@ -385,9 +386,14 @@
 
     def remote(role, x):
         if role == 1 and x < late:
-            units(role, "all", 0, 2 * rows, x, now=(spot[role, "all", 0, 2 * rows, x],))
+            for kind in ("own", "mate"):
+                units(role, kind, 0, rows, x, now=(spot[role, kind, 0, rows, x],))
             return
-        then = (spot[role, "all", rows, rows, y] for y in range(exp_dev)) if role > 1 and x == late else ()
+        then = ()
+        if 1 < role < far:
+            then = (spot[role, "all", rows, rows, x],)
+        elif role == far and x == late:
+            then = (spot[role, "all", rows, rows, y] for y in range(exp_dev))
         units(role, "all", 0, 2 * rows, x, now=(spot[role, "all", 0, rows, x],), then=then)
 
     def half(role, turn, side=None):
@@ -483,12 +489,15 @@
         out[:, cols] = full.astype(out.dtype)
 
     await_copy(x_buf.at[z, block(c), pl.ds(pl.multiple_of(d * own, own), own)], n_send, sent=True)
-    for q in range(chips):
-        await_copy(x_buf.at[q, block(c)], x_send.at[q, 0], sent=True)
-        for way, sends in ((1, jnp.logical_and(q <= z, z < chips - 1)), (2, jnp.logical_and(q >= z, z > 0))):
-            @pl.when(sends)
-            def _(q=q, way=way):
-                await_copy(x_buf.at[q, block(c)], x_send.at[q, way], sent=True)
+    await_copy(x_buf.at[:, block(c)], x_send.at[0], sent=True)
+    for place in range(chips):
+        @pl.when(z == place)
+        def _(place=place):
+            if place < chips - 1:
+                await_copy(x_buf.at[pl.ds(0, place + 1), block(c)], x_send.at[1], sent=True)
+            if place > 0:
+                await_copy(x_buf.at[pl.ds(place, chips - place), block(c)], x_send.at[2], sent=True)
+
     await_copy(hid.at[:, :, :, pl.ds(pl.multiple_of(d * ff, WIDE), ff)], h_send, sent=True)
     await_copy(pair_out.at[pl.ds(0, chips)], p_send, sent=True)
     await_copy(ret_out.at[pl.ds(1, chips - 1)], r_send, sent=True)
@@ -530,7 +539,7 @@
             pltpu.VMEM((chips, tiles, rows, WIDE), kind),
             dma((4,)),
             dma((exp_dev, 3)),
-            dma((chips, 3)),
+            dma((3,)),
             dma((chips, 2, 2)),
             dma((chips,)),
             dma((chips,)),

time: 46.2 us -> 46.1 us (level)
  no operation moved by 1% of the time
where the time goes in v4:
time: 46.1 us; the launch traced here: 45.7 us
  Pallas kernels  45.1 us (98%)
  local copies, waits for them, and re-layouts  0.66 us (1%)
    pallas_call x1, Pallas kernels, dense_on_device(): pl.pallas_call(functools.partial(dense_kernel, chips), out_shape=jax.Shap...  45.1 us

profile of v4, /device:TPU:0, one launch (start us, length us, event | category | flops | bytes accessed | tf_op | source)
XLA Modules:
  0.0 45.7 jit_solution(6250459749827026672)
XLA Ops:
  0.0 45.1 %shard_map.64 = bf16[64,1024]{1,0:T(8,128)(2,1)S(1)} custom-call(bf16[64,1024]{1,0:T(8,128)(2,1)} %tok_hbm.1, s32[8,64]{1,0:T(8,128)} %bitcast.2, s32[8,64]{1,0:T(8,128)} %bitcast.3, bf16[2,2048,768]{2,1,0:T(8,128)(2,1)} %gate_hbm.1, bf16[2,2048,768]{2,1,0:T(8,128)(2,1)} %up_hbm.1, bf16[2,1536,1024]{2,1,0:T(8,128)(2,1)} %down_hbm.1), custom_call_target="tpu_custom_call" | custom-call | flops 9663676416 | bytes 18874368 | tf_op jit(solution)/shard_map/pallas_call | solution.py:522
  45.1 0.7 %copy.8 = bf16[64,1024]{1,0:T(8,128)(2,1)} copy(bf16[64,1024]{1,0:T(8,128)(2,1)S(1)} %shard_map.64) | data formatting | bytes 262144
